TPU v7x, 512 devices: a whole 4x8x8 slice. The times are simulated.
512 devices in a mesh: vocab: 64 (over z, y), pipe: 8 (over x, core).
Axes of the slice: x: 4, y: 8, z: 8, core: 2. Of those that a mesh axis runs over, the one named last changes fastest.
Arguments:
- hidden_a: bfloat16 [2048, 4096], P('pipe', 'vocab'), parts along dimension 0, may hold values from -8 to 8, as said below
- labels_a: int32 [2048], P('pipe'), parts along dimension 0, may hold values from 0 to 32767
- hidden_b: bfloat16 [2048, 4096], P('pipe', 'vocab'), parts along dimension 0, may hold values from -8 to 8, as said below
- labels_b: int32 [2048], P('pipe'), parts along dimension 0, may hold values from 0 to 32767
- loss_cotangent: float32 [2048], P('pipe'), parts along dimension 0, may hold values from -192 to 192
- out_weight: bfloat16 [32768, 32768], P('pipe', 'vocab'), parts along dimension 0, may hold values from -0.28125 to 0.28125, as said below
Outputs:
- logits_a: bfloat16 [2048, 32768], P('pipe', 'vocab'), parts along dimension 0
- loss_a: float32 [2048], P('pipe'), parts along dimension 0
- amax_scale: float32 [8], P('pipe'), parts along dimension 0
- grad_hidden_b: bfloat16 [2048, 4096], P('pipe', 'vocab'), parts along dimension 0
There are 8 independent parts, one for each index of `pipe`. A program takes and returns all parts, laid end to end along the dimension named above; each array names one. Nothing has to cross between parts.
Inputs may be any that keep to these rules, and one draw needn't show every extreme that they name: `hidden_a`: hidden states of order one. `hidden_b`: hidden states of order one. `out_weight`: entries of scale 3 over the square root of 4096.
All inputs are finite; a program needn't handle non-finite values. Where the computation divides by a largest or mean magnitude, that divisor is 1e-20 or more.
Results may differ from a plain program's by a relative error of at most 0.0048.
Values may be sent and summed in bfloat16 or wider, within the bound.
No kernel may reach another device: no remote copies, remote signals or barrier semaphores. Data moves between devices by JAX's collectives and lax.ppermute only.
A program may use at most 64 MiB of HBM per device.

v0:
```python
import jax
import jax.numpy as jnp
from jax import lax
from jax.sharding import Mesh
from jax.sharding import PartitionSpec as P


Z, Y = ("z_two", "z_one"), ("y_two", "y_one")
VOCAB = (*Z, *Y)
LATTICE = ("z_two", "y_two")
FLIPS = ((1, 1), (1, 0), (0, 1))


def size(axes):
    return lax.axis_size(axes)


def from_everyone(x, axes):
    return lax.all_to_all(jnp.broadcast_to(x[None], (size(axes), *x.shape)), axes, 0, 0, tiled=True)


def neighbour(i, n, shift):
    return (i + 1 - 2 * ((i + shift) % 2) + n) % n


def exchanged(x, flip):
    shift = flip[0] * flip[1]
    nz, ny = size(Z), size(Y)
    pairs = []
    for z in range(nz):
        for y in range(ny):
            there = neighbour(z, nz, shift) if flip[0] else z, neighbour(y, ny, shift) if flip[1] else y
            pairs.append((z * ny + y, there[0] * ny + there[1]))
    return lax.ppermute(x, VOCAB, pairs)


def shards(hidden_a, labels_a, hidden_b, labels_b, loss_cotangent, out_weight):
    tokens, width = hidden_a.shape
    columns = out_weight.shape[1]
    offset = lax.axis_index(VOCAB) * columns
    lattice = size(LATTICE)
    half = lattice * width // 2
    by_class = out_weight.reshape(size(Z[0]), 2, size(Y[0]), 2, width, columns)

    def weight_rows(flip):
        z, y = lax.axis_index(Z[1]), lax.axis_index(Y[1])
        at = (0, z + flip[0] - 2 * z * flip[0], 0, y + flip[1] - 2 * y * flip[1], 0, 0)
        counts = (by_class.shape[0], 1, by_class.shape[2], 1, width, columns)
        return lax.dynamic_slice(by_class, at, counts).reshape(2 * half, columns)

    weights = {flip: weight_rows(flip) for flip in ((0, 0), *FLIPS)}

    def product(block, rows):
        return lax.dot_general(
            block, rows, (((0,), (0,)), ((), ())), preferred_element_type=jnp.float32
        )

    own = jnp.concatenate([hidden_b.T, hidden_a.T], axis=1)
    mine = from_everyone(own, LATTICE).reshape(2 * half, 2 * tokens)
    scores = product(mine, weights[0, 0])
    for flip in FLIPS:
        block = exchanged(mine, flip)
        scores = scores + product(block, weights[flip])
    scores_b, scores_a = scores[:tokens], scores[tokens:]
    column = offset + lax.broadcasted_iota(jnp.int32, (1, columns), 1)

    def log_total(scores):
        peak = jnp.max(scores, axis=1)
        return peak + jnp.log(jnp.sum(jnp.exp(scores - peak[:, None]), axis=1))

    label_own = jnp.sum(jnp.where(column == labels_a[:, None], scores_a, 0.0), axis=1)
    largest = jnp.full((128,), jnp.max(jnp.abs(scores_a)))
    line = jnp.concatenate([log_total(scores_b), log_total(scores_a), label_own, largest])
    lines = from_everyone(line.reshape(1, -1), VOCAB).reshape(-1, line.size)

    def joined(logs):
        peak = jnp.max(logs, axis=0)
        return peak + jnp.log(jnp.sum(jnp.exp(logs - peak), axis=0))

    log_b = joined(lines[:, :tokens])
    log_a = joined(lines[:, tokens : 2 * tokens])
    label_a = jnp.sum(lines[:, 2 * tokens : 3 * tokens], axis=0)
    loss_a = log_a - label_a
    amax_scale = (448.0 / jnp.max(lines[:, 3 * tokens :])).reshape(1).astype(jnp.float32)

    onehot = (column == labels_b[:, None]).astype(jnp.float32)
    dlogits_b = ((jnp.exp(scores_b - log_b[:, None]) - onehot) * loss_cotangent[:, None]).astype(
        jnp.bfloat16
    )

    def grad_rows(flip):
        return lax.dot_general(
            weights[flip], dlogits_b, (((1,), (1,)), ((), ())), preferred_element_type=jnp.float32
        )

    dlogits_b = lax.optimization_barrier(dlogits_b)
    total = lax.optimization_barrier(grad_rows((0, 0)))
    for flip in FLIPS:
        total = total + exchanged(grad_rows(flip).astype(jnp.bfloat16), flip).astype(jnp.float32)
    parts = total.astype(jnp.bfloat16).reshape(lattice, width, tokens)
    parts = lax.all_to_all(parts, LATTICE, 0, 0, tiled=True)
    grad_hidden_b = jnp.sum(parts.astype(jnp.float32), axis=0).astype(jnp.bfloat16).T
    return (scores_a.astype(jnp.bfloat16), loss_a, amax_scale, grad_hidden_b)


def solution(mesh):
    finer = Mesh(mesh.devices.reshape(4, 2, 4, 2, mesh.shape["pipe"]), (*VOCAB, "pipe"))
    placed = (P("pipe", VOCAB), P("pipe"), P("pipe", VOCAB), P("pipe"), P("pipe"), P("pipe", VOCAB))

    return jax.shard_map(
        shards,
        mesh=finer,
        in_specs=placed,
        out_specs=(P("pipe", VOCAB), P("pipe"), P("pipe"), P("pipe", VOCAB)),
        check_vma=False,
    )
```

profile of v0, /device:TPU:6, one launch (start us, length us, event | category | flops | bytes accessed | tf_op | source)
XLA Modules:
  0.0 154.5 jit_solution(11767959033108044854)
XLA Ops:
  0.6 0.8 pad_maximum_fusion
  1.4 0.1 broadcast_in_dim.10
  1.5 47.8 %all_to_all.15 = bf16[16,64,512]{2,1,0:T(8,128)(2,1)S(1)} all-to-all(bf16[16,64,512]{2,1,0:T(8,128)(2,1)S(1)} %broadcast_in_dim.10), channel_id=1, replica_groups=mesh['z_two'=4,'z_one'=2,'y_two'=4,'y_one'=2,'pipe'=8] {'z_two','y_two'}, dimensions={0} | all-to-all | bytes 2097152 | tf_op jit(solution)/shard_map/all_to_all | solution.py:19
  49.4 1.9 %collective-permute-start.2 = (bf16[1024,512]{1,0:T(8,128)(2,1)S(1)}, bf16[1024,512]{1,0:T(8,128)(2,1)S(1)}, u32[]{:S(2)}, u32[]{:S(2)}) collective-permute-start(bf16[1024,512]{1,0:T(8,128)(2,1)S(1)} %bitcast.42), channel_id=1, source_target_pairs={{0,8},{8,0},{16,24},{24,16},{32,40},{40,32},{48,56},{56,48},{64,72... | collective-permute-start | bytes 3145736 | tf_op jit(solution)/shard_map/ppermute | solution.py:34
  51.3 8.3 %collective-permute-start = (bf16[1024,512]{1,0:T(8,128)(2,1)S(1)}, bf16[1024,512]{1,0:T(8,128)(2,1)S(1)}, u32[]{:S(2)}, u32[]{:S(2)}) collective-permute-start(bf16[1024,512]{1,0:T(8,128)(2,1)S(1)} %bitcast.43), channel_id=1, source_target_pairs={{0,504},{8,464},{16,456},{24,480},{32,472},{40,496},{48,488},{56,4... | collective-permute-start | bytes 3145736 | tf_op jit(solution)/shard_map/ppermute | solution.py:34
  59.6 2.7 %constant_dynamic-slice_fusion.1 = (bf16[4,1,4,1,64,512]{5,4,3,2,1,0:T(8,128)(2,1)S(1)}, bf16[4,1,4,1,64,512]{5,4,3,2,1,0:T(8,128)(2,1)S(1)}, bf16[4,1,4,1,64,51...) fusion(bf16[4,2,4,2,64,512]{5,4,3,2,1,0:T(8,128)(2,1)} %bitcast.36, s32[]{:T(128)S(6)} %select_n.22, ...), kind=kLoop, calls=%fused_computation.30 | loop fusion | bytes 8388624 | tf_op jit(solution)/shard_map/dynamic_slice | solution.py:49
  62.3 1.9 %collective-permute-start.1 = (bf16[1024,512]{1,0:T(8,128)(2,1)S(1)}, bf16[1024,512]{1,0:T(8,128)(2,1)S(1)}, u32[]{:S(2)}, u32[]{:S(2)}) collective-permute-start(bf16[1024,512]{1,0:T(8,128)(2,1)S(1)} %bitcast.44), channel_id=1, source_target_pairs={{0,64},{8,72},{16,80},{24,88},{32,96},{40,104},{48,112},{56,120},{... | collective-permute-start | bytes 3145736 | tf_op jit(solution)/shard_map/ppermute | solution.py:34
  64.3 0.8 fusion.1
  65.0 9.8 %collective-permute-done.2 = bf16[1024,512]{1,0:T(8,128)(2,1)S(1)} collective-permute-done((bf16[1024,512]{1,0:T(8,128)(2,1)S(1)}, bf16[1024,512]{1,0:T(8,128)(2,1)S(1)}, u32[]{:S(2)}, u32[]{:S(2)}) %collective-permute-start.2) | collective-permute-done | bytes 1048608 | tf_op jit(solution)/shard_map/ppermute | solution.py:34
  74.9 0.8 fusion.2
  75.6 6.3 %collective-permute-done = bf16[1024,512]{1,0:T(8,128)(2,1)S(1)} collective-permute-done((bf16[1024,512]{1,0:T(8,128)(2,1)S(1)}, bf16[1024,512]{1,0:T(8,128)(2,1)S(1)}, u32[]{:S(2)}, u32[]{:S(2)}) %collective-permute-start) | collective-permute-done | bytes 1048608 | tf_op jit(solution)/shard_map/ppermute | solution.py:34
  81.9 0.0 copy-start
  81.9 0.8 convolution_add_fusion.1
  82.7 5.3 %collective-permute-done.1 = bf16[1024,512]{1,0:T(8,128)(2,1)S(1)} collective-permute-done((bf16[1024,512]{1,0:T(8,128)(2,1)S(1)}, bf16[1024,512]{1,0:T(8,128)(2,1)S(1)}, u32[]{:S(2)}, u32[]{:S(2)}) %collective-permute-start.1) | collective-permute-done | bytes 1048608 | tf_op jit(solution)/shard_map/ppermute | solution.py:34
  88.0 0.0 copy-start.1
  88.0 0.0 copy-start.2
  88.0 0.8 fusion
  88.8 0.1 slice_reduce_fusion
  88.8 0.0 copy-done
  88.8 0.7 exponential_reduce_fusion.1
  89.5 0.1 exponential_reduce_fusion
  89.7 0.6 broadcast_in_dim.12
  90.3 0.1 broadcast_in_dim.13
  90.5 19.0 %all_to_all.16 = f32[64,1,896]{2,1,0:T(1,128)S(1)} all-to-all(f32[64,1,896]{2,1,0:T(1,128)S(1)} %broadcast_in_dim.13), channel_id=1, replica_groups=mesh['z_two'=4,'z_one'=2,'y_two'=4,'y_one'=2,'pipe'=8] {'z_two','z_one',..., dimensions={0} | all-to-all | bytes 458752 | tf_op jit(solution)/shard_map/all_to_all | solution.py:19
  109.5 0.0 copy-done.1
  109.5 0.0 copy-done.2
  109.6 0.2 multiply_convert_fusion
  109.7 0.4 convolution_convert_fusion.2
  110.2 0.4 convolution_convert_fusion.1
  110.6 0.4 convolution_convert_fusion
  111.0 2.5 %collective-permute-start.3 = (bf16[1024,256]{1,0:T(8,128)(2,1)S(1)}, bf16[1024,256]{1,0:T(8,128)(2,1)S(1)}, u32[]{:S(2)}, u32[]{:S(2)}) collective-permute-start(bf16[1024,256]{1,0:T(8,128)(2,1)S(1)} %convolution_convert_fusion.2), channel_id=1, source_target_pairs={{0,504},{8,464},{16,456},{24,480},{32,472},{40,496},{48,488},{56,4... | collective-permute-start | bytes 1572872 | tf_op jit(solution)/shard_map/ppermute | solution.py:34
  113.5 3.0 %collective-permute-start.4 = (bf16[1024,256]{1,0:T(8,128)(2,1)S(1)}, bf16[1024,256]{1,0:T(8,128)(2,1)S(1)}, u32[]{:S(2)}, u32[]{:S(2)}) collective-permute-start(bf16[1024,256]{1,0:T(8,128)(2,1)S(1)} %convolution_convert_fusion.1), channel_id=1, source_target_pairs={{0,64},{8,72},{16,80},{24,88},{32,96},{40,104},{48,112},{56,120},{... | collective-permute-start | bytes 1572872 | tf_op jit(solution)/shard_map/ppermute | solution.py:34
  116.5 2.5 %collective-permute-start.5 = (bf16[1024,256]{1,0:T(8,128)(2,1)S(1)}, bf16[1024,256]{1,0:T(8,128)(2,1)S(1)}, u32[]{:S(2)}, u32[]{:S(2)}) collective-permute-start(bf16[1024,256]{1,0:T(8,128)(2,1)S(1)} %convolution_convert_fusion), channel_id=1, source_target_pairs={{0,8},{8,0},{16,24},{24,16},{32,40},{40,32},{48,56},{56,48},{64,72... | collective-permute-start | bytes 1572872 | tf_op jit(solution)/shard_map/ppermute | solution.py:34
  119.1 0.4 fusion.3
  119.5 7.4 %collective-permute-done.3 = bf16[1024,256]{1,0:T(8,128)(2,1)S(1)} collective-permute-done((bf16[1024,256]{1,0:T(8,128)(2,1)S(1)}, bf16[1024,256]{1,0:T(8,128)(2,1)S(1)}, u32[]{:S(2)}, u32[]{:S(2)}) %collective-permute-start.3) | collective-permute-done | bytes 524320 | tf_op jit(solution)/shard_map/ppermute | solution.py:34
  126.9 0.0 collective-permute-done.4
  126.9 1.8 %collective-permute-done.5 = bf16[1024,256]{1,0:T(8,128)(2,1)S(1)} collective-permute-done((bf16[1024,256]{1,0:T(8,128)(2,1)S(1)}, bf16[1024,256]{1,0:T(8,128)(2,1)S(1)}, u32[]{:S(2)}, u32[]{:S(2)}) %collective-permute-start.5) | collective-permute-done | bytes 524320 | tf_op jit(solution)/shard_map/ppermute | solution.py:34
  128.7 1.1 add_convert_fusion
  129.8 7.3 %all-to-all-start.2 = ((bf16[16,64,256]{2,1,0:T(8,128)(2,1)}), bf16[16,64,256]{2,1,0:T(8,128)(2,1)S(1)}, u32[]{:S(2)}, u32[]{:S(2)}) async-start(bf16[16,64,256]{2,1,0:T(8,128)(2,1)} %bitcast.9), calls=%async_computation.2 | async-start | bytes 1048576 | tf_op jit(solution)/shard_map/all_to_all | solution.py:101
  137.2 0.8 copy.12
  138.0 0.6 slice_reduce_fusion.5
  139.3 0.6 add_subtract_fusion
  139.9 12.8 %all-to-all-done.2 = bf16[16,64,256]{2,1,0:T(8,128)(2,1)S(1)} async-done(((bf16[16,64,256]{2,1,0:T(8,128)(2,1)}), bf16[16,64,256]{2,1,0:T(8,128)(2,1)S(1)}, u32[]{:S(2)}, u32[]{:S(2)}) %all-to-all-start.2) | async-done | bytes 524320 | tf_op jit(solution)/shard_map/all_to_all | solution.py:101
  152.7 0.7 reduce_sum.72
  (8 shorter events, 0.2 us)
Async XLA Ops:
  49.4 25.5 %collective-permute-start.2 = (bf16[1024,512]{1,0:T(8,128)(2,1)S(1)}, bf16[1024,512]{1,0:T(8,128)(2,1)S(1)}, u32[]{:S(2)}, u32[]{:S(2)}) collective-permute-start(bf16[1024,512]{1,0:T(8,128)(2,1)S(1)} %bitcast.42), channel_id=1, source_target_pairs={{0,8},{8,0},{16,24},{24,16},{32,40},{40,32},{48,56},{56,48},{64,72... | collective-permute-start | bytes 3145736 | tf_op jit(solution)/shard_map/ppermute | solution.py:34
  51.3 30.6 %collective-permute-start = (bf16[1024,512]{1,0:T(8,128)(2,1)S(1)}, bf16[1024,512]{1,0:T(8,128)(2,1)S(1)}, u32[]{:S(2)}, u32[]{:S(2)}) collective-permute-start(bf16[1024,512]{1,0:T(8,128)(2,1)S(1)} %bitcast.43), channel_id=1, source_target_pairs={{0,504},{8,464},{16,456},{24,480},{32,472},{40,496},{48,488},{56,4... | collective-permute-start | bytes 3145736 | tf_op jit(solution)/shard_map/ppermute | solution.py:34
  62.3 25.7 %collective-permute-start.1 = (bf16[1024,512]{1,0:T(8,128)(2,1)S(1)}, bf16[1024,512]{1,0:T(8,128)(2,1)S(1)}, u32[]{:S(2)}, u32[]{:S(2)}) collective-permute-start(bf16[1024,512]{1,0:T(8,128)(2,1)S(1)} %bitcast.44), channel_id=1, source_target_pairs={{0,64},{8,72},{16,80},{24,88},{32,96},{40,104},{48,112},{56,120},{... | collective-permute-start | bytes 3145736 | tf_op jit(solution)/shard_map/ppermute | solution.py:34
  81.9 6.9 %copy-start = (s32[256]{0:T(256)S(1)}, s32[256]{0:T(256)}, u32[]{:S(2)}) copy-start(s32[256]{0:T(256)} %param.7) | copy-start | bytes 3076
  88.0 21.6 %copy-start.1 = (f32[256]{0:T(256)S(1)}, f32[256]{0:T(256)}, u32[]{:S(2)}) copy-start(f32[256]{0:T(256)} %param.10) | copy-start | bytes 3076
  88.0 21.6 %copy-start.2 = (s32[256]{0:T(256)S(1)}, s32[256]{0:T(256)}, u32[]{:S(2)}) copy-start(s32[256]{0:T(256)} %param.9) | copy-start | bytes 3076
  111.0 15.9 %collective-permute-start.3 = (bf16[1024,256]{1,0:T(8,128)(2,1)S(1)}, bf16[1024,256]{1,0:T(8,128)(2,1)S(1)}, u32[]{:S(2)}, u32[]{:S(2)}) collective-permute-start(bf16[1024,256]{1,0:T(8,128)(2,1)S(1)} %convolution_convert_fusion.2), channel_id=1, source_target_pairs={{0,504},{8,464},{16,456},{24,480},{32,472},{40,496},{48,488},{56,4... | collective-permute-start | bytes 1572872 | tf_op jit(solution)/shard_map/ppermute | solution.py:34
  113.5 13.4 %collective-permute-start.4 = (bf16[1024,256]{1,0:T(8,128)(2,1)S(1)}, bf16[1024,256]{1,0:T(8,128)(2,1)S(1)}, u32[]{:S(2)}, u32[]{:S(2)}) collective-permute-start(bf16[1024,256]{1,0:T(8,128)(2,1)S(1)} %convolution_convert_fusion.1), channel_id=1, source_target_pairs={{0,64},{8,72},{16,80},{24,88},{32,96},{40,104},{48,112},{56,120},{... | collective-permute-start | bytes 1572872 | tf_op jit(solution)/shard_map/ppermute | solution.py:34
  116.5 12.2 %collective-permute-start.5 = (bf16[1024,256]{1,0:T(8,128)(2,1)S(1)}, bf16[1024,256]{1,0:T(8,128)(2,1)S(1)}, u32[]{:S(2)}, u32[]{:S(2)}) collective-permute-start(bf16[1024,256]{1,0:T(8,128)(2,1)S(1)} %convolution_convert_fusion), channel_id=1, source_target_pairs={{0,8},{8,0},{16,24},{24,16},{32,40},{40,32},{48,56},{56,48},{64,72... | collective-permute-start | bytes 1572872 | tf_op jit(solution)/shard_map/ppermute | solution.py:34
  129.8 22.9 %all-to-all-start.2 = ((bf16[16,64,256]{2,1,0:T(8,128)(2,1)}), bf16[16,64,256]{2,1,0:T(8,128)(2,1)S(1)}, u32[]{:S(2)}, u32[]{:S(2)}) async-start(bf16[16,64,256]{2,1,0:T(8,128)(2,1)} %bitcast.9), calls=%async_computation.2 | async-start | bytes 1048576 | tf_op jit(solution)/shard_map/all_to_all | solution.py:101
where the time goes:
time: 155 us
  blocking collectives  66.8 us (43%)
  waiting for transfers between devices  43.5 us (28%)
  starting transfers between devices  27.5 us (18%)
  other arithmetic  4.86 us (3%)
  matrix products  4.76 us (3%)
  local copies, waits for them, and re-layouts  4.45 us (3%)
  between operations  2.68 us (2%)
    all_to_all x2, blocking collectives, from_everyone(): lax.all_to_all(jnp.broadcast_to(x[None], (size(axes), *x.shape)), axes, 0...  66.8 us
    ppermute x6, waiting for transfers between devices, exchanged(): return lax.ppermute(x, VOCAB, pairs)  30.7 us
    ppermute x6, starting transfers between devices, exchanged(): return lax.ppermute(x, VOCAB, pairs)  20.2 us
    all_to_all x1, waiting for transfers between devices, shards(): parts = lax.all_to_all(parts, LATTICE, 0, 0, tiled=True)  12.8 us
    all_to_all x1, starting transfers between devices, shards(): parts = lax.all_to_all(parts, LATTICE, 0, 0, tiled=True)  7.31 us
  transfers between devices with their start and end apart: 7, of which 6 were waited for; matrix products, arithmetic and copies ran while one was open for 5% of the time, Pallas kernels for 0%

commit v1 on v0

--- a/solution.py
+++ b/solution.py
@@ -7,7 +7,7 @@
 
 Z, Y = ("z_two", "z_one"), ("y_two", "y_one")
 VOCAB = (*Z, *Y)
-LATTICE = ("z_two", "y_two")
+LATTICE, QUAD = ("z_two", "y_two"), ("z_one", "y_one")
 FLIPS = ((1, 1), (1, 0), (0, 1))
 
 
@@ -57,49 +57,64 @@
 
     own = jnp.concatenate([hidden_b.T, hidden_a.T], axis=1)
     mine = from_everyone(own, LATTICE).reshape(2 * half, 2 * tokens)
-    scores = product(mine, weights[0, 0])
-    for flip in FLIPS:
-        block = exchanged(mine, flip)
-        scores = scores + product(block, weights[flip])
-    scores_b, scores_a = scores[:tokens], scores[tokens:]
+
+    def scores_of(mine):
+        scores = product(mine, weights[0, 0])
+        for flip in FLIPS:
+            block = exchanged(mine, flip)
+            scores = scores + product(block, weights[flip])
+        return scores
+
+    scores_b = scores_of(mine[:, :tokens])
+    scores_a = scores_of(mine[:, tokens:])
     column = offset + lax.broadcasted_iota(jnp.int32, (1, columns), 1)
+    column_a = lax.optimization_barrier(column)
 
     def log_total(scores):
         peak = jnp.max(scores, axis=1)
         return peak + jnp.log(jnp.sum(jnp.exp(scores - peak[:, None]), axis=1))
 
-    label_own = jnp.sum(jnp.where(column == labels_a[:, None], scores_a, 0.0), axis=1)
-    largest = jnp.full((128,), jnp.max(jnp.abs(scores_a)))
-    line = jnp.concatenate([log_total(scores_b), log_total(scores_a), label_own, largest])
-    lines = from_everyone(line.reshape(1, -1), VOCAB).reshape(-1, line.size)
-
     def joined(logs):
         peak = jnp.max(logs, axis=0)
         return peak + jnp.log(jnp.sum(jnp.exp(logs - peak), axis=0))
 
-    log_b = joined(lines[:, :tokens])
-    log_a = joined(lines[:, tokens : 2 * tokens])
-    label_a = jnp.sum(lines[:, 2 * tokens : 3 * tokens], axis=0)
-    loss_a = log_a - label_a
-    amax_scale = (448.0 / jnp.max(lines[:, 3 * tokens :])).reshape(1).astype(jnp.float32)
+    log_b = joined(from_everyone(log_total(scores_b).reshape(1, -1), VOCAB).reshape(-1, tokens))
+    label_own = jnp.sum(jnp.where(column_a == labels_a[:, None], scores_a, 0.0), axis=1)
+    largest = jnp.broadcast_to(jnp.max(jnp.abs(scores_a)), (tokens,))
+    lines = jnp.stack([log_total(scores_a), label_own, largest])
+
+    def joined_lines(lines):
+        return jnp.stack(
+            [joined(lines[:, 0]), jnp.sum(lines[:, 1], axis=0), jnp.max(lines[:, 2], axis=0)]
+        )
+
+    quad = joined_lines(from_everyone(lines, QUAD).reshape(-1, *lines.shape))
+    high = lax.reduce_precision(quad, 8, 7)
+    riders = jnp.concatenate([high, quad - high, jnp.zeros_like(quad[:2])]).astype(jnp.bfloat16)
 
     onehot = (column == labels_b[:, None]).astype(jnp.float32)
     dlogits_b = ((jnp.exp(scores_b - log_b[:, None]) - onehot) * loss_cotangent[:, None]).astype(
         jnp.bfloat16
     )
 
+    dlogits_b = lax.optimization_barrier(dlogits_b)
+
     def grad_rows(flip):
         return lax.dot_general(
             weights[flip], dlogits_b, (((1,), (1,)), ((), ())), preferred_element_type=jnp.float32
         )
 
-    dlogits_b = lax.optimization_barrier(dlogits_b)
     total = lax.optimization_barrier(grad_rows((0, 0)))
     for flip in FLIPS:
         total = total + exchanged(grad_rows(flip).astype(jnp.bfloat16), flip).astype(jnp.float32)
     parts = total.astype(jnp.bfloat16).reshape(lattice, width, tokens)
+    parts = jnp.concatenate([parts, jnp.broadcast_to(riders[None], (lattice, *riders.shape))], axis=1)
     parts = lax.all_to_all(parts, LATTICE, 0, 0, tiled=True)
-    grad_hidden_b = jnp.sum(parts.astype(jnp.float32), axis=0).astype(jnp.bfloat16).T
+    grad_hidden_b = jnp.sum(parts[:, :width].astype(jnp.float32), axis=0).astype(jnp.bfloat16).T
+    came = parts[:, width : width + 6].astype(jnp.float32)
+    log_a, label_a, largest = joined_lines(came[:, :3] + came[:, 3:])
+    loss_a = log_a - label_a
+    amax_scale = (448.0 / largest[:1]).astype(jnp.float32)
     return (scores_a.astype(jnp.bfloat16), loss_a, amax_scale, grad_hidden_b)
 
 

time: 155 us -> 161 us (1.039)
  blocking collectives: 66.8 us -> 21.3 us
  starting transfers between devices: 27.5 us -> 57.1 us
  waiting for transfers between devices: 43.5 us -> 51.4 us
  matrix products: 4.76 us -> 11.7 us
  local copies, waits for them, and re-layouts: 4.45 us -> 10.3 us
    all_to_all x2 -> x1, blocking collectives: 66.8 us -> 21.3 us  [shards(): parts = lax.all_to_all(parts, LATTICE, 0, 0, tiled=True)]
    all_to_all x1 -> x3, waiting for transfers between devices: 12.8 us -> 40 us  [from_everyone(): lax.all_to_all(jnp.broadcast_to(x[None], (size(axes), *x.shape)), axes, 0...]
    all_to_all x1 -> x3, starting transfers between devices: 7.31 us -> 28.4 us  [from_everyone(): lax.all_to_all(jnp.broadcast_to(x[None], (size(axes), *x.shape)), axes, 0...]
    ppermute x6 -> x9, waiting for transfers between devices: 30.7 us -> 11.4 us  [exchanged(): return lax.ppermute(x, VOCAB, pairs)]
    ppermute x6 -> x9, starting transfers between devices: 20.2 us -> 28.7 us  [exchanged(): return lax.ppermute(x, VOCAB, pairs)]
    dot_general x4 -> x8, matrix products: 3.02 us -> 9.87 us  [product(): lax.dot_general(block, rows, (((0,), (0,)), ((), ())), preferred_element_...]
    slice x1 -> x2, local copies, waits for them, and re-layouts: 0.04 us -> 2.67 us  [the longest x1 2.15 us: shards(): scores_b = scores_of(mine[:, :tokens])]
    broadcast_in_dim x2 -> x3, local copies, waits for them, and re-layouts: 0.21 us -> 2.35 us  [from_everyone(): jnp.broadcast_to(x[None], (size(axes), *x.shape))]
  transfers between devices with their start and end apart: 7 -> 12, of which waited for: 6 -> 5; matrix products, arithmetic and copies ran while one was open for 5% -> 11% of each run, Pallas kernels for 0% -> 0%
where the time goes in v1:
time: 161 us; the launch traced here: 160 us
  starting transfers between devices  57.1 us (35%)
  waiting for transfers between devices  51.4 us (32%)
  blocking collectives  21.3 us (13%)
  matrix products  11.7 us (7%)
  local copies, waits for them, and re-layouts  10.3 us (6%)
  other arithmetic  5.81 us (4%)
  between operations  2.83 us (2%)
    all_to_all x3, waiting for transfers between devices, from_everyone(): lax.all_to_all(jnp.broadcast_to(x[None], (size(axes), *x.shape)), axes, 0...  40 us
    ppermute x9, starting transfers between devices, exchanged(): return lax.ppermute(x, VOCAB, pairs)  28.7 us
    all_to_all x3, starting transfers between devices, from_everyone(): lax.all_to_all(jnp.broadcast_to(x[None], (size(axes), *x.shape)), axes, 0...  28.4 us
    all_to_all x1, blocking collectives, shards(): parts = lax.all_to_all(parts, LATTICE, 0, 0, tiled=True)  21.3 us
    ppermute x9, waiting for transfers between devices, exchanged(): return lax.ppermute(x, VOCAB, pairs)  11.4 us
    dot_general x8, matrix products, product(): lax.dot_general(block, rows, (((0,), (0,)), ((), ())), preferred_element_...  9.87 us
    dynamic_slice x1, local copies, waits for them, and re-layouts, weight_rows(): return lax.dynamic_slice(by_class, at, counts).reshape(2 * half, columns)  3.55 us
  transfers between devices with their start and end apart: 12, of which 5 were waited for; matrix products, arithmetic and copies ran while one was open for 11% of the time, Pallas kernels for 0%

profile of v1, /device:TPU:6, one launch (start us, length us, event | category | flops | bytes accessed | tf_op | source)
XLA Modules:
  0.0 160.5 jit_solution(2119435899460128779)
XLA Ops:
  0.6 0.8 pad_maximum_fusion.1
  1.4 1.1 broadcast_in_dim.14
  2.5 15.7 %all-to-all-start = ((bf16[16,64,512]{2,1,0:T(8,128)(2,1)}), bf16[16,64,512]{2,1,0:T(8,128)(2,1)}, u32[]{:S(2)}, u32[]{:S(2)}) async-start(bf16[16,64,512]{2,1,0:T(8,128)(2,1)} %broadcast_in_dim.14), calls=%async_computation | async-start | bytes 2097152 | tf_op jit(solution)/shard_map/all_to_all | solution.py:19
  18.3 0.1 pad.4.clone
  18.4 3.5 %constant_dynamic-slice_fusion.1 = (bf16[4,1,4,1,64,512]{5,4,3,2,1,0:T(8,128)(2,1)S(1)}, bf16[4,1,4,1,64,512]{5,4,3,2,1,0:T(8,128)(2,1)S(1)}, bf16[4,1,4,1,64,51...) fusion(bf16[4,2,4,2,64,512]{5,4,3,2,1,0:T(8,128)(2,1)} %bitcast.66, s32[]{:T(128)S(6)} %select_n.22, ...), kind=kLoop, calls=%fused_computation.47 | loop fusion | bytes 8388624 | tf_op jit(solution)/shard_map/dynamic_slice | solution.py:49
  21.9 27.8 %all-to-all-done = bf16[16,64,512]{2,1,0:T(8,128)(2,1)} async-done(((bf16[16,64,512]{2,1,0:T(8,128)(2,1)}), bf16[16,64,512]{2,1,0:T(8,128)(2,1)}, u32[]{:S(2)}, u32[]{:S(2)}) %all-to-all-start) | async-done | bytes 1048608 | tf_op jit(solution)/shard_map/all_to_all | solution.py:19
  49.7 2.2 %fusion.13 = (bf16[1024,256]{1,0:T(8,128)(2,1)}, bf16[1024,256]{1,0:T(8,128)(2,1)S(1)}) fusion(bf16[1024,512]{1,0:T(8,128)(2,1)} %bitcast.2), kind=kLoop, calls=%fused_computation.56 | loop fusion | bytes 2097152 | tf_op jit(solution)/shard_map/slice | solution.py:68
  51.9 1.9 %collective-permute-start.2 = (bf16[1024,256]{1,0:T(8,128)(2,1)S(1)}, bf16[1024,256]{1,0:T(8,128)(2,1)S(1)}, u32[]{:S(2)}, u32[]{:S(2)}) collective-permute-start(bf16[1024,256]{1,0:T(8,128)(2,1)S(1)} %get-tuple-element.18), channel_id=1, source_target_pairs={{0,8},{8,0},{16,24},{24,16},{32,40},{40,32},{48,56},{56,48},{64,72... | collective-permute-start | bytes 1572872 | tf_op jit(solution)/shard_map/ppermute | solution.py:34
  53.8 9.5 %collective-permute-start = (bf16[1024,256]{1,0:T(8,128)(2,1)S(1)}, bf16[1024,256]{1,0:T(8,128)(2,1)S(1)}, u32[]{:S(2)}, u32[]{:S(2)}) collective-permute-start(bf16[1024,256]{1,0:T(8,128)(2,1)S(1)} %get-tuple-element.18), channel_id=1, source_target_pairs={{0,504},{8,464},{16,456},{24,480},{32,472},{40,496},{48,488},{56,4... | collective-permute-start | bytes 1572872 | tf_op jit(solution)/shard_map/ppermute | solution.py:34
  63.3 1.9 %collective-permute-start.1 = (bf16[1024,256]{1,0:T(8,128)(2,1)S(1)}, bf16[1024,256]{1,0:T(8,128)(2,1)S(1)}, u32[]{:S(2)}, u32[]{:S(2)}) collective-permute-start(bf16[1024,256]{1,0:T(8,128)(2,1)S(1)} %get-tuple-element.18), channel_id=1, source_target_pairs={{0,64},{8,72},{16,80},{24,88},{32,96},{40,104},{48,112},{56,120},{... | collective-permute-start | bytes 1572872 | tf_op jit(solution)/shard_map/ppermute | solution.py:34
  65.2 1.9 %collective-permute-start.5 = (bf16[1024,256]{1,0:T(8,128)(2,1)}, bf16[1024,256]{1,0:T(8,128)(2,1)}, u32[]{:S(2)}, u32[]{:S(2)}) collective-permute-start(bf16[1024,256]{1,0:T(8,128)(2,1)} %get-tuple-element.17), channel_id=1, source_target_pairs={{0,8},{8,0},{16,24},{24,16},{32,40},{40,32},{48,56},{56,48},{64,72... | collective-permute-start | bytes 1572872 | tf_op jit(solution)/shard_map/ppermute | solution.py:34
  67.2 1.9 %collective-permute-start.3 = (bf16[1024,256]{1,0:T(8,128)(2,1)}, bf16[1024,256]{1,0:T(8,128)(2,1)}, u32[]{:S(2)}, u32[]{:S(2)}) collective-permute-start(bf16[1024,256]{1,0:T(8,128)(2,1)} %get-tuple-element.17), channel_id=1, source_target_pairs={{0,504},{8,464},{16,456},{24,480},{32,472},{40,496},{48,488},{56,4... | collective-permute-start | bytes 1572872 | tf_op jit(solution)/shard_map/ppermute | solution.py:34
  69.1 0.0 copy-done.1
  69.1 1.5 fusion.11
  70.6 2.3 %fusion.9 = f32[256,512]{1,0:T(8,128)} fusion(bf16[1024,512]{1,0:T(8,128)(2,1)S(1)} %bitcast.68, bf16[1024,512]{1,0:T(8,128)(2,1)} %bitcast.2), kind=kOutput, calls=%fused_computation.52 | convolution fusion | flops 268435456 | bytes 2097152 | tf_op jit(solution)/shard_map/dot_general | solution.py:54
  72.9 0.0 collective-permute-done.2
  72.9 3.9 %collective-permute-start.4 = (bf16[1024,256]{1,0:T(8,128)(2,1)}, bf16[1024,256]{1,0:T(8,128)(2,1)}, u32[]{:S(2)}, u32[]{:S(2)}) collective-permute-start(bf16[1024,256]{1,0:T(8,128)(2,1)} %get-tuple-element.17), channel_id=1, source_target_pairs={{0,64},{8,72},{16,80},{24,88},{32,96},{40,104},{48,112},{56,120},{... | collective-permute-start | bytes 1572872 | tf_op jit(solution)/shard_map/ppermute | solution.py:34
  76.8 0.4 fusion.16
  77.3 0.0 collective-permute-done
  77.3 0.5 convolution_add_fusion.3
  77.8 0.0 collective-permute-done.1
  77.8 0.0 copy-start.4
  77.8 0.5 fusion.14
  78.3 0.1 copy-done.4
  78.5 1.5 abs_reduce_fusion
  80.0 0.7 pad.10.clone
  80.7 0.1 maximum_maximum_fusion
  80.8 0.6 broadcast_in_dim.17
  81.4 3.3 %all-to-all-start.2 = ((f32[4,3,256]{2,1,0:T(4,128)}), f32[4,3,256]{2,1,0:T(4,128)S(1)}, u32[]{:S(2)}, u32[]{:S(2)}) async-start(f32[4,3,256]{2,1,0:T(4,128)} %broadcast_in_dim.17), calls=%async_computation.2 | async-start | bytes 32768 | tf_op jit(solution)/shard_map/all_to_all | solution.py:19
  84.7 0.0 collective-permute-done.5
  84.7 1.5 fusion.17
  86.2 0.0 collective-permute-done.3
  86.3 0.0 copy-done.3
  86.3 1.5 convolution_add_fusion.1
  87.8 0.0 copy-start.5
  87.8 0.0 copy-start.6
  87.8 0.0 collective-permute-done.4
  87.8 1.6 fusion.15
  89.4 0.8 copy-done
  90.2 0.2 exponential_reduce_fusion.1
  90.4 0.0 all-to-all-done.2
  90.5 0.7 broadcast_in_dim.15
  91.1 9.4 %all-to-all-start.1 = ((f32[64,1,256]{2,1,0:T(1,128)}), f32[64,1,256]{2,1,0:T(1,128)S(1)}, u32[]{:S(2)}, u32[]{:S(2)}) async-start(f32[64,1,256]{2,1,0:T(1,128)} %broadcast_in_dim.15), calls=%async_computation.1 | async-start | bytes 131072 | tf_op jit(solution)/shard_map/all_to_all | solution.py:19
  100.6 12.2 %all-to-all-done.1 = f32[64,1,256]{2,1,0:T(1,128)S(1)} async-done(((f32[64,1,256]{2,1,0:T(1,128)}), f32[64,1,256]{2,1,0:T(1,128)S(1)}, u32[]{:S(2)}, u32[]{:S(2)}) %all-to-all-start.1) | async-done | bytes 65568 | tf_op jit(solution)/shard_map/all_to_all | solution.py:19
  112.8 0.1 reduce_max.73
  112.9 1.2 multiply_convert_fusion
  114.2 0.5 convolution_convert_fusion
  114.6 0.5 convolution_convert_fusion.1
  115.1 0.0 copy-start.2
  115.1 0.5 convolution_convert_fusion.2
  115.6 2.6 %collective-permute-start.8 = (bf16[1024,256]{1,0:T(8,128)(2,1)S(1)}, bf16[1024,256]{1,0:T(8,128)(2,1)S(1)}, u32[]{:S(2)}, u32[]{:S(2)}) collective-permute-start(bf16[1024,256]{1,0:T(8,128)(2,1)S(1)} %convolution_convert_fusion), channel_id=1, source_target_pairs={{0,8},{8,0},{16,24},{24,16},{32,40},{40,32},{48,56},{56,48},{64,72... | collective-permute-start | bytes 1572872 | tf_op jit(solution)/shard_map/ppermute | solution.py:34
  118.2 2.6 %collective-permute-start.7 = (bf16[1024,256]{1,0:T(8,128)(2,1)S(1)}, bf16[1024,256]{1,0:T(8,128)(2,1)S(1)}, u32[]{:S(2)}, u32[]{:S(2)}) collective-permute-start(bf16[1024,256]{1,0:T(8,128)(2,1)S(1)} %convolution_convert_fusion.1), channel_id=1, source_target_pairs={{0,64},{8,72},{16,80},{24,88},{32,96},{40,104},{48,112},{56,120},{... | collective-permute-start | bytes 1572872 | tf_op jit(solution)/shard_map/ppermute | solution.py:34
  120.8 2.4 %collective-permute-start.6 = (bf16[1024,256]{1,0:T(8,128)(2,1)S(1)}, bf16[1024,256]{1,0:T(8,128)(2,1)S(1)}, u32[]{:S(2)}, u32[]{:S(2)}) collective-permute-start(bf16[1024,256]{1,0:T(8,128)(2,1)S(1)} %convolution_convert_fusion.2), channel_id=1, source_target_pairs={{0,504},{8,464},{16,456},{24,480},{32,472},{40,496},{48,488},{56,4... | collective-permute-start | bytes 1572872 | tf_op jit(solution)/shard_map/ppermute | solution.py:34
  123.2 0.1 maximum_maximum_fusion.1
  123.3 0.5 fusion.18
  123.8 3.3 %collective-permute-done.8 = bf16[1024,256]{1,0:T(8,128)(2,1)S(1)} collective-permute-done((bf16[1024,256]{1,0:T(8,128)(2,1)S(1)}, bf16[1024,256]{1,0:T(8,128)(2,1)S(1)}, u32[]{:S(2)}, u32[]{:S(2)}) %collective-permute-start.8) | collective-permute-done | bytes 524320 | tf_op jit(solution)/shard_map/ppermute | solution.py:34
  127.1 2.4 %collective-permute-done.7 = bf16[1024,256]{1,0:T(8,128)(2,1)S(1)} collective-permute-done((bf16[1024,256]{1,0:T(8,128)(2,1)S(1)}, bf16[1024,256]{1,0:T(8,128)(2,1)S(1)}, u32[]{:S(2)}, u32[]{:S(2)}) %collective-permute-start.7) | collective-permute-done | bytes 524320 | tf_op jit(solution)/shard_map/ppermute | solution.py:34
  129.5 5.7 %collective-permute-done.6 = bf16[1024,256]{1,0:T(8,128)(2,1)S(1)} collective-permute-done((bf16[1024,256]{1,0:T(8,128)(2,1)S(1)}, bf16[1024,256]{1,0:T(8,128)(2,1)S(1)}, u32[]{:S(2)}, u32[]{:S(2)}) %collective-permute-start.6) | collective-permute-done | bytes 524320 | tf_op jit(solution)/shard_map/ppermute | solution.py:34
  135.2 0.2 add_convert_fusion
  135.5 21.3 %all_to_all.20 = bf16[16,72,256]{2,1,0:T(8,128)(2,1)S(1)} all-to-all(bf16[16,72,256]{2,1,0:T(8,128)(2,1)S(1)} %pad_maximum_fusion), channel_id=1, replica_groups=mesh['z_two'=4,'z_one'=2,'y_two'=4,'y_one'=2,'pipe'=8] {'z_two','y_two'}, dimensions={0} | all-to-all | bytes 1179648 | tf_op jit(solution)/shard_map/all_to_all | solution.py:112
  156.8 0.1 slice_reduce_fusion.1
  156.9 0.5 slice.50
  157.4 0.6 add_subtract_fusion
  158.7 0.7 slice_reduce_fusion
  (22 shorter events, 0.3 us)
Async XLA Ops:
  2.5 47.2 %all-to-all-start = ((bf16[16,64,512]{2,1,0:T(8,128)(2,1)}), bf16[16,64,512]{2,1,0:T(8,128)(2,1)}, u32[]{:S(2)}, u32[]{:S(2)}) async-start(bf16[16,64,512]{2,1,0:T(8,128)(2,1)} %broadcast_in_dim.14), calls=%async_computation | async-start | bytes 2097152 | tf_op jit(solution)/shard_map/all_to_all | solution.py:19
  49.7 19.4 %copy-start.1 = (bf16[4,1,4,1,64,512]{5,4,3,2,1,0:T(8,128)(2,1)S(1)}, bf16[4,1,4,1,64,512]{5,4,3,2,1,0:T(8,128)(2,1)}, u32[]{:S(2)}) copy-start(bf16[4,1,4,1,64,512]{5,4,3,2,1,0:T(8,128)(2,1)} %get-tuple-element.16) | copy-start | bytes 3145732
  51.9 21.0 %collective-permute-start.2 = (bf16[1024,256]{1,0:T(8,128)(2,1)S(1)}, bf16[1024,256]{1,0:T(8,128)(2,1)S(1)}, u32[]{:S(2)}, u32[]{:S(2)}) collective-permute-start(bf16[1024,256]{1,0:T(8,128)(2,1)S(1)} %get-tuple-element.18), channel_id=1, source_target_pairs={{0,8},{8,0},{16,24},{24,16},{32,40},{40,32},{48,56},{56,48},{64,72... | collective-permute-start | bytes 1572872 | tf_op jit(solution)/shard_map/ppermute | solution.py:34
  53.8 23.5 %collective-permute-start = (bf16[1024,256]{1,0:T(8,128)(2,1)S(1)}, bf16[1024,256]{1,0:T(8,128)(2,1)S(1)}, u32[]{:S(2)}, u32[]{:S(2)}) collective-permute-start(bf16[1024,256]{1,0:T(8,128)(2,1)S(1)} %get-tuple-element.18), channel_id=1, source_target_pairs={{0,504},{8,464},{16,456},{24,480},{32,472},{40,496},{48,488},{56,4... | collective-permute-start | bytes 1572872 | tf_op jit(solution)/shard_map/ppermute | solution.py:34
  63.3 14.5 %collective-permute-start.1 = (bf16[1024,256]{1,0:T(8,128)(2,1)S(1)}, bf16[1024,256]{1,0:T(8,128)(2,1)S(1)}, u32[]{:S(2)}, u32[]{:S(2)}) collective-permute-start(bf16[1024,256]{1,0:T(8,128)(2,1)S(1)} %get-tuple-element.18), channel_id=1, source_target_pairs={{0,64},{8,72},{16,80},{24,88},{32,96},{40,104},{48,112},{56,120},{... | collective-permute-start | bytes 1572872 | tf_op jit(solution)/shard_map/ppermute | solution.py:34
  65.2 19.5 %collective-permute-start.5 = (bf16[1024,256]{1,0:T(8,128)(2,1)}, bf16[1024,256]{1,0:T(8,128)(2,1)}, u32[]{:S(2)}, u32[]{:S(2)}) collective-permute-start(bf16[1024,256]{1,0:T(8,128)(2,1)} %get-tuple-element.17), channel_id=1, source_target_pairs={{0,8},{8,0},{16,24},{24,16},{32,40},{40,32},{48,56},{56,48},{64,72... | collective-permute-start | bytes 1572872 | tf_op jit(solution)/shard_map/ppermute | solution.py:34
  67.2 19.1 %collective-permute-start.3 = (bf16[1024,256]{1,0:T(8,128)(2,1)}, bf16[1024,256]{1,0:T(8,128)(2,1)}, u32[]{:S(2)}, u32[]{:S(2)}) collective-permute-start(bf16[1024,256]{1,0:T(8,128)(2,1)} %get-tuple-element.17), channel_id=1, source_target_pairs={{0,504},{8,464},{16,456},{24,480},{32,472},{40,496},{48,488},{56,4... | collective-permute-start | bytes 1572872 | tf_op jit(solution)/shard_map/ppermute | solution.py:34
  72.9 14.9 %collective-permute-start.4 = (bf16[1024,256]{1,0:T(8,128)(2,1)}, bf16[1024,256]{1,0:T(8,128)(2,1)}, u32[]{:S(2)}, u32[]{:S(2)}) collective-permute-start(bf16[1024,256]{1,0:T(8,128)(2,1)} %get-tuple-element.17), channel_id=1, source_target_pairs={{0,64},{8,72},{16,80},{24,88},{32,96},{40,104},{48,112},{56,120},{... | collective-permute-start | bytes 1572872 | tf_op jit(solution)/shard_map/ppermute | solution.py:34
  77.8 0.7 copy-start.4
  81.4 9.0 %all-to-all-start.2 = ((f32[4,3,256]{2,1,0:T(4,128)}), f32[4,3,256]{2,1,0:T(4,128)S(1)}, u32[]{:S(2)}, u32[]{:S(2)}) async-start(f32[4,3,256]{2,1,0:T(4,128)} %broadcast_in_dim.17), calls=%async_computation.2 | async-start | bytes 32768 | tf_op jit(solution)/shard_map/all_to_all | solution.py:19
  84.7 1.6 copy-start.3
  87.8 25.1 %copy-start.5 = (f32[256]{0:T(256)S(1)}, f32[256]{0:T(256)}, u32[]{:S(2)}) copy-start(f32[256]{0:T(256)} %param.10) | copy-start | bytes 3076
  87.8 25.1 %copy-start.6 = (s32[256]{0:T(256)S(1)}, s32[256]{0:T(256)}, u32[]{:S(2)}) copy-start(s32[256]{0:T(256)} %param.9) | copy-start | bytes 3076
  89.4 0.8 copy-start
  91.1 21.6 %all-to-all-start.1 = ((f32[64,1,256]{2,1,0:T(1,128)}), f32[64,1,256]{2,1,0:T(1,128)S(1)}, u32[]{:S(2)}, u32[]{:S(2)}) async-start(f32[64,1,256]{2,1,0:T(1,128)} %broadcast_in_dim.15), calls=%async_computation.1 | async-start | bytes 131072 | tf_op jit(solution)/shard_map/all_to_all | solution.py:19
  115.1 8.2 %copy-start.2 = (bf16[4,1,4,1,64,512]{5,4,3,2,1,0:T(8,128)(2,1)S(1)}, bf16[4,1,4,1,64,512]{5,4,3,2,1,0:T(8,128)(2,1)}, u32[]{:S(2)}) copy-start(bf16[4,1,4,1,64,512]{5,4,3,2,1,0:T(8,128)(2,1)} %get-tuple-element.16) | copy-start | bytes 3145732
  115.6 11.5 %collective-permute-start.8 = (bf16[1024,256]{1,0:T(8,128)(2,1)S(1)}, bf16[1024,256]{1,0:T(8,128)(2,1)S(1)}, u32[]{:S(2)}, u32[]{:S(2)}) collective-permute-start(bf16[1024,256]{1,0:T(8,128)(2,1)S(1)} %convolution_convert_fusion), channel_id=1, source_target_pairs={{0,8},{8,0},{16,24},{24,16},{32,40},{40,32},{48,56},{56,48},{64,72... | collective-permute-start | bytes 1572872 | tf_op jit(solution)/shard_map/ppermute | solution.py:34
  118.2 11.3 %collective-permute-start.7 = (bf16[1024,256]{1,0:T(8,128)(2,1)S(1)}, bf16[1024,256]{1,0:T(8,128)(2,1)S(1)}, u32[]{:S(2)}, u32[]{:S(2)}) collective-permute-start(bf16[1024,256]{1,0:T(8,128)(2,1)S(1)} %convolution_convert_fusion.1), channel_id=1, source_target_pairs={{0,64},{8,72},{16,80},{24,88},{32,96},{40,104},{48,112},{56,120},{... | collective-permute-start | bytes 1572872 | tf_op jit(solution)/shard_map/ppermute | solution.py:34
  120.8 14.4 %collective-permute-start.6 = (bf16[1024,256]{1,0:T(8,128)(2,1)S(1)}, bf16[1024,256]{1,0:T(8,128)(2,1)S(1)}, u32[]{:S(2)}, u32[]{:S(2)}) collective-permute-start(bf16[1024,256]{1,0:T(8,128)(2,1)S(1)} %convolution_convert_fusion.2), channel_id=1, source_target_pairs={{0,504},{8,464},{16,456},{24,480},{32,472},{40,496},{48,488},{56,4... | collective-permute-start | bytes 1572872 | tf_op jit(solution)/shard_map/ppermute | solution.py:34

commit v2 on v1

--- a/solution.py
+++ b/solution.py
@@ -62,10 +62,10 @@
         scores = product(mine, weights[0, 0])
         for flip in FLIPS:
             block = exchanged(mine, flip)
-            scores = scores + product(block, weights[flip])
+            scores = lax.optimization_barrier(scores) + product(block, weights[flip])
         return scores
 
-    scores_b = scores_of(mine[:, :tokens])
+    scores_b = scores_of(lax.optimization_barrier(mine[:, :tokens]))
     scores_a = scores_of(mine[:, tokens:])
     column = offset + lax.broadcasted_iota(jnp.int32, (1, columns), 1)
     column_a = lax.optimization_barrier(column)
@@ -90,7 +90,7 @@
 
     quad = joined_lines(from_everyone(lines, QUAD).reshape(-1, *lines.shape))
     high = lax.reduce_precision(quad, 8, 7)
-    riders = jnp.concatenate([high, quad - high, jnp.zeros_like(quad[:2])]).astype(jnp.bfloat16)
+    riders = jnp.concatenate([high, quad - high, high[:2]]).astype(jnp.bfloat16)
 
     onehot = (column == labels_b[:, None]).astype(jnp.float32)
     dlogits_b = ((jnp.exp(scores_b - log_b[:, None]) - onehot) * loss_cotangent[:, None]).astype(

time: 161 us -> 162 us (level)
  the two profiles are of different devices: /device:TPU:6 before, /device:TPU:2 now
where the time goes in v2:
time: 162 us; the launch traced here: 161 us
  starting transfers between devices  57.1 us (35%)
  waiting for transfers between devices  51.5 us (32%)
  blocking collectives  21.3 us (13%)
  matrix products  11.6 us (7%)
  local copies, waits for them, and re-layouts  10.7 us (7%)
  other arithmetic  6.19 us (4%)
  between operations  2.88 us (2%)
    all_to_all x3, waiting for transfers between devices, from_everyone(): lax.all_to_all(jnp.broadcast_to(x[None], (size(axes), *x.shape)), axes, 0...  40.1 us
    all_to_all x3, starting transfers between devices, from_everyone(): lax.all_to_all(jnp.broadcast_to(x[None], (size(axes), *x.shape)), axes, 0...  30.2 us
    ppermute x9, starting transfers between devices, exchanged(): return lax.ppermute(x, VOCAB, pairs)  27 us
    all_to_all x1, blocking collectives, shards(): parts = lax.all_to_all(parts, LATTICE, 0, 0, tiled=True)  21.3 us
    ppermute x9, waiting for transfers between devices, exchanged(): return lax.ppermute(x, VOCAB, pairs)  11.4 us
    dot_general x8, matrix products, product(): lax.dot_general(block, rows, (((0,), (0,)), ((), ())), preferred_element_...  9.79 us
    dynamic_slice x1, local copies, waits for them, and re-layouts, weight_rows(): return lax.dynamic_slice(by_class, at, counts).reshape(2 * half, columns)  3.57 us
  transfers between devices with their start and end apart: 12, of which 5 were waited for; matrix products, arithmetic and copies ran while one was open for 11% of the time, Pallas kernels for 0%

profile of v2, /device:TPU:2, one launch (start us, length us, event | category | flops | bytes accessed | tf_op | source)
XLA Modules:
  0.0 161.3 jit_solution(12714577269748832784)
XLA Ops:
  0.6 0.8 pad_maximum_fusion.1
  1.4 1.1 broadcast_in_dim.12
  2.5 15.7 %all-to-all-start = ((bf16[16,64,512]{2,1,0:T(8,128)(2,1)}), bf16[16,64,512]{2,1,0:T(8,128)(2,1)}, u32[]{:S(2)}, u32[]{:S(2)}) async-start(bf16[16,64,512]{2,1,0:T(8,128)(2,1)} %broadcast_in_dim.12), calls=%async_computation | async-start | bytes 2097152 | tf_op jit(solution)/shard_map/all_to_all | solution.py:19
  18.3 3.6 %constant_dynamic-slice_fusion = (bf16[4,1,4,1,64,512]{5,4,3,2,1,0:T(8,128)(2,1)S(1)}, bf16[4,1,4,1,64,512]{5,4,3,2,1,0:T(8,128)(2,1)S(1)}, bf16[4,1,4,1,64,512]...) fusion(bf16[4,2,4,2,64,512]{5,4,3,2,1,0:T(8,128)(2,1)} %bitcast.70, s32[]{:T(128)S(6)} %select_n.20, ...), kind=kLoop, calls=%fused_computation.42 | loop fusion | bytes 8388624 | tf_op jit(solution)/shard_map/dynamic_slice | solution.py:49
  21.9 27.9 %all-to-all-done = bf16[16,64,512]{2,1,0:T(8,128)(2,1)} async-done(((bf16[16,64,512]{2,1,0:T(8,128)(2,1)}), bf16[16,64,512]{2,1,0:T(8,128)(2,1)}, u32[]{:S(2)}, u32[]{:S(2)}) %all-to-all-start) | async-done | bytes 1048608 | tf_op jit(solution)/shard_map/all_to_all | solution.py:19
  49.7 2.2 %fusion.11 = (bf16[1024,256]{1,0:T(8,128)(2,1)}, bf16[1024,256]{1,0:T(8,128)(2,1)S(1)}) fusion(bf16[1024,512]{1,0:T(8,128)(2,1)} %bitcast.2), kind=kLoop, calls=%fused_computation.52 | loop fusion | bytes 2097152 | tf_op jit(solution)/shard_map/slice | solution.py:68
  51.9 4.6 %collective-permute-start = (bf16[1024,256]{1,0:T(8,128)(2,1)S(1)}, bf16[1024,256]{1,0:T(8,128)(2,1)S(1)}, u32[]{:S(2)}, u32[]{:S(2)}) collective-permute-start(bf16[1024,256]{1,0:T(8,128)(2,1)S(1)} %get-tuple-element.22), channel_id=1, source_target_pairs={{0,504},{8,464},{16,456},{24,480},{32,472},{40,496},{48,488},{56,4... | collective-permute-start | bytes 1572872 | tf_op jit(solution)/shard_map/ppermute | solution.py:34
  56.5 1.9 %collective-permute-start.1 = (bf16[1024,256]{1,0:T(8,128)(2,1)S(1)}, bf16[1024,256]{1,0:T(8,128)(2,1)S(1)}, u32[]{:S(2)}, u32[]{:S(2)}) collective-permute-start(bf16[1024,256]{1,0:T(8,128)(2,1)S(1)} %get-tuple-element.22), channel_id=1, source_target_pairs={{0,64},{8,72},{16,80},{24,88},{32,96},{40,104},{48,112},{56,120},{... | collective-permute-start | bytes 1572872 | tf_op jit(solution)/shard_map/ppermute | solution.py:34
  58.5 4.6 %collective-permute-start.2 = (bf16[1024,256]{1,0:T(8,128)(2,1)S(1)}, bf16[1024,256]{1,0:T(8,128)(2,1)S(1)}, u32[]{:S(2)}, u32[]{:S(2)}) collective-permute-start(bf16[1024,256]{1,0:T(8,128)(2,1)S(1)} %get-tuple-element.22), channel_id=1, source_target_pairs={{0,8},{8,0},{16,24},{24,16},{32,40},{40,32},{48,56},{56,48},{64,72... | collective-permute-start | bytes 1572872 | tf_op jit(solution)/shard_map/ppermute | solution.py:34
  63.1 4.1 %collective-permute-start.3 = (bf16[1024,256]{1,0:T(8,128)(2,1)}, bf16[1024,256]{1,0:T(8,128)(2,1)}, u32[]{:S(2)}, u32[]{:S(2)}) collective-permute-start(bf16[1024,256]{1,0:T(8,128)(2,1)} %get-tuple-element.21), channel_id=1, source_target_pairs={{0,504},{8,464},{16,456},{24,480},{32,472},{40,496},{48,488},{56,4... | collective-permute-start | bytes 1572872 | tf_op jit(solution)/shard_map/ppermute | solution.py:34
  67.2 2.2 %collective-permute-start.4 = (bf16[1024,256]{1,0:T(8,128)(2,1)}, bf16[1024,256]{1,0:T(8,128)(2,1)}, u32[]{:S(2)}, u32[]{:S(2)}) collective-permute-start(bf16[1024,256]{1,0:T(8,128)(2,1)} %get-tuple-element.21), channel_id=1, source_target_pairs={{0,64},{8,72},{16,80},{24,88},{32,96},{40,104},{48,112},{56,120},{... | collective-permute-start | bytes 1572872 | tf_op jit(solution)/shard_map/ppermute | solution.py:34
  69.4 0.0 copy-done
  69.4 1.5 fusion.7
  70.9 2.3 %fusion.14 = f32[256,512]{1,0:T(8,128)} fusion(bf16[1024,256]{1,0:T(8,128)(2,1)} %get-tuple-element.21, bf16[1024,512]{1,0:T(8,128)(2,1)S(1)} %bitcast.68), kind=kOutput, calls=%fused_computation.55 | convolution fusion | flops 268435456 | bytes 2097152 | tf_op jit(solution)/shard_map/dot_general | solution.py:54
  73.2 0.0 collective-permute-done
  73.2 1.9 %collective-permute-start.5 = (bf16[1024,256]{1,0:T(8,128)(2,1)}, bf16[1024,256]{1,0:T(8,128)(2,1)}, u32[]{:S(2)}, u32[]{:S(2)}) collective-permute-start(bf16[1024,256]{1,0:T(8,128)(2,1)} %get-tuple-element.21), channel_id=1, source_target_pairs={{0,8},{8,0},{16,24},{24,16},{32,40},{40,32},{48,56},{56,48},{64,72... | collective-permute-start | bytes 1572872 | tf_op jit(solution)/shard_map/ppermute | solution.py:34
  75.1 0.5 convolution_add_fusion.1
  75.6 0.0 collective-permute-done.1
  75.6 0.4 fusion.12
  76.0 0.1 add.132
  76.1 0.0 collective-permute-done.2
  76.1 0.4 fusion.13
  76.6 0.0 copy-start.3
  76.6 0.1 fusion.10
  76.7 0.5 copy-done.3
  77.3 1.5 abs_reduce_fusion
  78.8 0.7 pad.10.clone
  79.5 0.1 maximum_maximum_fusion
  79.6 0.6 broadcast_in_dim.15
  80.2 4.5 %all-to-all-start.2 = ((f32[4,3,256]{2,1,0:T(4,128)}), f32[4,3,256]{2,1,0:T(4,128)S(1)}, u32[]{:S(2)}, u32[]{:S(2)}) async-start(f32[4,3,256]{2,1,0:T(4,128)} %broadcast_in_dim.15), calls=%async_computation.2 | async-start | bytes 32768 | tf_op jit(solution)/shard_map/all_to_all | solution.py:19
  84.7 0.0 collective-permute-done.3
  84.7 1.7 %convolution_add_fusion = f32[256,512]{1,0:T(8,128)S(1)} fusion(f32[256,512]{1,0:T(8,128)} %fusion.14, bf16[1024,256]{1,0:T(8,128)(2,1)} %collective-permute-done.3, bf16[1024,512]{1,0:T(8,128)(2,1)S(1)} %bitcast.59), kind=kOutput, calls=%fused_computation.3 | convolution fusion | flops 268566528 | bytes 2621440 | tf_op jit(solution)/shard_map/dot_general | solution.py:54
  86.3 0.0 collective-permute-done.4
  86.4 1.5 fusion.15
  87.9 0.1 add.135
  87.9 0.0 collective-permute-done.5
  88.0 1.5 fusion.16
  89.5 0.0 copy-start.4
  89.5 0.0 copy-start.5
  89.5 0.1 fusion.9
  89.6 0.8 copy-done.2
  90.4 0.2 exponential_reduce_fusion.1
  90.7 0.0 all-to-all-done.2
  90.7 0.7 broadcast_in_dim.13
  91.3 10.0 %all-to-all-start.1 = ((f32[64,1,256]{2,1,0:T(1,128)}), f32[64,1,256]{2,1,0:T(1,128)S(1)}, u32[]{:S(2)}, u32[]{:S(2)}) async-start(f32[64,1,256]{2,1,0:T(1,128)} %broadcast_in_dim.13), calls=%async_computation.1 | async-start | bytes 131072 | tf_op jit(solution)/shard_map/all_to_all | solution.py:19
  101.4 12.2 %all-to-all-done.1 = f32[64,1,256]{2,1,0:T(1,128)S(1)} async-done(((f32[64,1,256]{2,1,0:T(1,128)}), f32[64,1,256]{2,1,0:T(1,128)S(1)}, u32[]{:S(2)}, u32[]{:S(2)}) %all-to-all-start.1) | async-done | bytes 65568 | tf_op jit(solution)/shard_map/all_to_all | solution.py:19
  113.5 0.1 reduce_max.73
  113.7 1.2 multiply_convert_fusion
  114.9 0.5 convolution_convert_fusion
  115.4 0.5 convolution_convert_fusion.1
  115.9 0.5 convolution_convert_fusion.2
  116.3 2.6 %collective-permute-start.8 = (bf16[1024,256]{1,0:T(8,128)(2,1)S(1)}, bf16[1024,256]{1,0:T(8,128)(2,1)S(1)}, u32[]{:S(2)}, u32[]{:S(2)}) collective-permute-start(bf16[1024,256]{1,0:T(8,128)(2,1)S(1)} %convolution_convert_fusion), channel_id=1, source_target_pairs={{0,8},{8,0},{16,24},{24,16},{32,40},{40,32},{48,56},{56,48},{64,72... | collective-permute-start | bytes 1572872 | tf_op jit(solution)/shard_map/ppermute | solution.py:34
  119.0 2.6 %collective-permute-start.7 = (bf16[1024,256]{1,0:T(8,128)(2,1)S(1)}, bf16[1024,256]{1,0:T(8,128)(2,1)S(1)}, u32[]{:S(2)}, u32[]{:S(2)}) collective-permute-start(bf16[1024,256]{1,0:T(8,128)(2,1)S(1)} %convolution_convert_fusion.1), channel_id=1, source_target_pairs={{0,64},{8,72},{16,80},{24,88},{32,96},{40,104},{48,112},{56,120},{... | collective-permute-start | bytes 1572872 | tf_op jit(solution)/shard_map/ppermute | solution.py:34
  121.5 2.4 %collective-permute-start.6 = (bf16[1024,256]{1,0:T(8,128)(2,1)S(1)}, bf16[1024,256]{1,0:T(8,128)(2,1)S(1)}, u32[]{:S(2)}, u32[]{:S(2)}) collective-permute-start(bf16[1024,256]{1,0:T(8,128)(2,1)S(1)} %convolution_convert_fusion.2), channel_id=1, source_target_pairs={{0,504},{8,464},{16,456},{24,480},{32,472},{40,496},{48,488},{56,4... | collective-permute-start | bytes 1572872 | tf_op jit(solution)/shard_map/ppermute | solution.py:34
  124.1 0.5 fusion.17
  124.5 3.4 %collective-permute-done.8 = bf16[1024,256]{1,0:T(8,128)(2,1)S(1)} collective-permute-done((bf16[1024,256]{1,0:T(8,128)(2,1)S(1)}, bf16[1024,256]{1,0:T(8,128)(2,1)S(1)}, u32[]{:S(2)}, u32[]{:S(2)}) %collective-permute-start.8) | collective-permute-done | bytes 524320 | tf_op jit(solution)/shard_map/ppermute | solution.py:34
  127.9 2.4 %collective-permute-done.7 = bf16[1024,256]{1,0:T(8,128)(2,1)S(1)} collective-permute-done((bf16[1024,256]{1,0:T(8,128)(2,1)S(1)}, bf16[1024,256]{1,0:T(8,128)(2,1)S(1)}, u32[]{:S(2)}, u32[]{:S(2)}) %collective-permute-start.7) | collective-permute-done | bytes 524320 | tf_op jit(solution)/shard_map/ppermute | solution.py:34
  130.3 5.7 %collective-permute-done.6 = bf16[1024,256]{1,0:T(8,128)(2,1)S(1)} collective-permute-done((bf16[1024,256]{1,0:T(8,128)(2,1)S(1)}, bf16[1024,256]{1,0:T(8,128)(2,1)S(1)}, u32[]{:S(2)}, u32[]{:S(2)}) %collective-permute-start.6) | collective-permute-done | bytes 524320 | tf_op jit(solution)/shard_map/ppermute | solution.py:34
  135.9 0.2 add_convert_fusion
  136.2 21.3 %all_to_all.20 = bf16[16,72,256]{2,1,0:T(8,128)(2,1)S(1)} all-to-all(bf16[16,72,256]{2,1,0:T(8,128)(2,1)S(1)} %pad_maximum_fusion), channel_id=1, replica_groups=mesh['z_two'=4,'z_one'=2,'y_two'=4,'y_one'=2,'pipe'=8] {'z_two','y_two'}, dimensions={0} | all-to-all | bytes 1179648 | tf_op jit(solution)/shard_map/all_to_all | solution.py:112
  157.6 0.1 slice_reduce_fusion.1
  157.6 0.5 slice.55
  158.2 0.6 add_subtract_fusion
  159.4 0.7 slice_reduce_fusion
  (23 shorter events, 0.3 us)
Async XLA Ops:
  2.5 47.2 %all-to-all-start = ((bf16[16,64,512]{2,1,0:T(8,128)(2,1)}), bf16[16,64,512]{2,1,0:T(8,128)(2,1)}, u32[]{:S(2)}, u32[]{:S(2)}) async-start(bf16[16,64,512]{2,1,0:T(8,128)(2,1)} %broadcast_in_dim.12), calls=%async_computation | async-start | bytes 2097152 | tf_op jit(solution)/shard_map/all_to_all | solution.py:19
  49.7 19.6 %copy-start = (bf16[4,1,4,1,64,512]{5,4,3,2,1,0:T(8,128)(2,1)S(1)}, bf16[4,1,4,1,64,512]{5,4,3,2,1,0:T(8,128)(2,1)}, u32[]{:S(2)}) copy-start(bf16[4,1,4,1,64,512]{5,4,3,2,1,0:T(8,128)(2,1)} %get-tuple-element.20) | copy-start | bytes 3145732
  51.9 21.3 %collective-permute-start = (bf16[1024,256]{1,0:T(8,128)(2,1)S(1)}, bf16[1024,256]{1,0:T(8,128)(2,1)S(1)}, u32[]{:S(2)}, u32[]{:S(2)}) collective-permute-start(bf16[1024,256]{1,0:T(8,128)(2,1)S(1)} %get-tuple-element.22), channel_id=1, source_target_pairs={{0,504},{8,464},{16,456},{24,480},{32,472},{40,496},{48,488},{56,4... | collective-permute-start | bytes 1572872 | tf_op jit(solution)/shard_map/ppermute | solution.py:34
  56.5 19.0 %collective-permute-start.1 = (bf16[1024,256]{1,0:T(8,128)(2,1)S(1)}, bf16[1024,256]{1,0:T(8,128)(2,1)S(1)}, u32[]{:S(2)}, u32[]{:S(2)}) collective-permute-start(bf16[1024,256]{1,0:T(8,128)(2,1)S(1)} %get-tuple-element.22), channel_id=1, source_target_pairs={{0,64},{8,72},{16,80},{24,88},{32,96},{40,104},{48,112},{56,120},{... | collective-permute-start | bytes 1572872 | tf_op jit(solution)/shard_map/ppermute | solution.py:34
  58.5 17.7 %collective-permute-start.2 = (bf16[1024,256]{1,0:T(8,128)(2,1)S(1)}, bf16[1024,256]{1,0:T(8,128)(2,1)S(1)}, u32[]{:S(2)}, u32[]{:S(2)}) collective-permute-start(bf16[1024,256]{1,0:T(8,128)(2,1)S(1)} %get-tuple-element.22), channel_id=1, source_target_pairs={{0,8},{8,0},{16,24},{24,16},{32,40},{40,32},{48,56},{56,48},{64,72... | collective-permute-start | bytes 1572872 | tf_op jit(solution)/shard_map/ppermute | solution.py:34
  63.1 21.6 %collective-permute-start.3 = (bf16[1024,256]{1,0:T(8,128)(2,1)}, bf16[1024,256]{1,0:T(8,128)(2,1)}, u32[]{:S(2)}, u32[]{:S(2)}) collective-permute-start(bf16[1024,256]{1,0:T(8,128)(2,1)} %get-tuple-element.21), channel_id=1, source_target_pairs={{0,504},{8,464},{16,456},{24,480},{32,472},{40,496},{48,488},{56,4... | collective-permute-start | bytes 1572872 | tf_op jit(solution)/shard_map/ppermute | solution.py:34
  67.2 19.2 %collective-permute-start.4 = (bf16[1024,256]{1,0:T(8,128)(2,1)}, bf16[1024,256]{1,0:T(8,128)(2,1)}, u32[]{:S(2)}, u32[]{:S(2)}) collective-permute-start(bf16[1024,256]{1,0:T(8,128)(2,1)} %get-tuple-element.21), channel_id=1, source_target_pairs={{0,64},{8,72},{16,80},{24,88},{32,96},{40,104},{48,112},{56,120},{... | collective-permute-start | bytes 1572872 | tf_op jit(solution)/shard_map/ppermute | solution.py:34
  73.2 14.8 %collective-permute-start.5 = (bf16[1024,256]{1,0:T(8,128)(2,1)}, bf16[1024,256]{1,0:T(8,128)(2,1)}, u32[]{:S(2)}, u32[]{:S(2)}) collective-permute-start(bf16[1024,256]{1,0:T(8,128)(2,1)} %get-tuple-element.21), channel_id=1, source_target_pairs={{0,8},{8,0},{16,24},{24,16},{32,40},{40,32},{48,56},{56,48},{64,72... | collective-permute-start | bytes 1572872 | tf_op jit(solution)/shard_map/ppermute | solution.py:34
  76.6 0.7 copy-start.3
  80.2 10.5 %all-to-all-start.2 = ((f32[4,3,256]{2,1,0:T(4,128)}), f32[4,3,256]{2,1,0:T(4,128)S(1)}, u32[]{:S(2)}, u32[]{:S(2)}) async-start(f32[4,3,256]{2,1,0:T(4,128)} %broadcast_in_dim.15), calls=%async_computation.2 | async-start | bytes 32768 | tf_op jit(solution)/shard_map/all_to_all | solution.py:19
  89.5 24.2 %copy-start.4 = (f32[256]{0:T(256)S(1)}, f32[256]{0:T(256)}, u32[]{:S(2)}) copy-start(f32[256]{0:T(256)} %param.10) | copy-start | bytes 3076
  89.5 24.2 %copy-start.5 = (s32[256]{0:T(256)S(1)}, s32[256]{0:T(256)}, u32[]{:S(2)}) copy-start(s32[256]{0:T(256)} %param.9) | copy-start | bytes 3076
  89.6 0.8 copy-start.2
  91.3 22.2 %all-to-all-start.1 = ((f32[64,1,256]{2,1,0:T(1,128)}), f32[64,1,256]{2,1,0:T(1,128)S(1)}, u32[]{:S(2)}, u32[]{:S(2)}) async-start(f32[64,1,256]{2,1,0:T(1,128)} %broadcast_in_dim.13), calls=%async_computation.1 | async-start | bytes 131072 | tf_op jit(solution)/shard_map/all_to_all | solution.py:19
  115.9 8.2 %copy-start.1 = (bf16[4,1,4,1,64,512]{5,4,3,2,1,0:T(8,128)(2,1)S(1)}, bf16[4,1,4,1,64,512]{5,4,3,2,1,0:T(8,128)(2,1)}, u32[]{:S(2)}) copy-start(bf16[4,1,4,1,64,512]{5,4,3,2,1,0:T(8,128)(2,1)} %get-tuple-element.20) | copy-start | bytes 3145732
  116.3 11.5 %collective-permute-start.8 = (bf16[1024,256]{1,0:T(8,128)(2,1)S(1)}, bf16[1024,256]{1,0:T(8,128)(2,1)S(1)}, u32[]{:S(2)}, u32[]{:S(2)}) collective-permute-start(bf16[1024,256]{1,0:T(8,128)(2,1)S(1)} %convolution_convert_fusion), channel_id=1, source_target_pairs={{0,8},{8,0},{16,24},{24,16},{32,40},{40,32},{48,56},{56,48},{64,72... | collective-permute-start | bytes 1572872 | tf_op jit(solution)/shard_map/ppermute | solution.py:34
  119.0 11.3 %collective-permute-start.7 = (bf16[1024,256]{1,0:T(8,128)(2,1)S(1)}, bf16[1024,256]{1,0:T(8,128)(2,1)S(1)}, u32[]{:S(2)}, u32[]{:S(2)}) collective-permute-start(bf16[1024,256]{1,0:T(8,128)(2,1)S(1)} %convolution_convert_fusion.1), channel_id=1, source_target_pairs={{0,64},{8,72},{16,80},{24,88},{32,96},{40,104},{48,112},{56,120},{... | collective-permute-start | bytes 1572872 | tf_op jit(solution)/shard_map/ppermute | solution.py:34
  121.5 14.4 %collective-permute-start.6 = (bf16[1024,256]{1,0:T(8,128)(2,1)S(1)}, bf16[1024,256]{1,0:T(8,128)(2,1)S(1)}, u32[]{:S(2)}, u32[]{:S(2)}) collective-permute-start(bf16[1024,256]{1,0:T(8,128)(2,1)S(1)} %convolution_convert_fusion.2), channel_id=1, source_target_pairs={{0,504},{8,464},{16,456},{24,480},{32,472},{40,496},{48,488},{56,4... | collective-permute-start | bytes 1572872 | tf_op jit(solution)/shard_map/ppermute | solution.py:34
